TPU v7x, 32 devices: a whole 2x2x4 slice. The times are simulated.
32 devices in a mesh: dp: 8 (over y, x, core), tensor: 4 (over z).
Axes of the slice: x: 2, y: 2, z: 4, core: 2. Of those that a mesh axis runs over, the one named last changes fastest.
Arguments:
- activations: bfloat16 [3072, 16384], P(('dp', 'tensor')), may hold values from -6 to 6
- out_grad: bfloat16 [3072, 16384], P('dp', 'tensor'), may hold values from -0.25 to 0.25
- block_ids: int32 [4, 12], replicated, may hold values from 0 to 127, as said below
- owner_map: int32 [8, 4], replicated, may hold values from 0 to 1, as said below
- master: float32 [1024, 16384], P('dp', 'tensor'), may hold values from -3 to 3
- moment: float32 [1024, 16384], P('dp', 'tensor'), may hold values from -3 to 3
- second: float32 [1024, 16384], P('dp', 'tensor'), may hold values from 0.01 to 2
Outputs:
- new_master: float32 [1024, 16384], P('dp', 'tensor')
- new_moment: float32 [1024, 16384], P('dp', 'tensor')
- new_second: float32 [1024, 16384], P('dp', 'tensor')
- hot_weights: bfloat16 [1024, 16384], P('dp')
- cold_recv: float32 [4096, 16384], P('dp', 'tensor')
Inputs may be any that keep to these rules, and one draw needn't show every extreme that they name: `block_ids`: the 12 block numbers in a row are distinct. `owner_map`: each row has between 1 and 3 ones; some row has exactly 3 ones and some row exactly 1.
All inputs are finite; a program needn't handle non-finite values.
Results may differ from a plain program's by a relative error of at most 0.006.
Values may be sent and summed in bfloat16 or wider, within the bound.
A program may use at most 128 MiB of HBM per device.

v0:
```python
import jax
import jax.numpy as jnp
from jax import lax
from jax.sharding import PartitionSpec as P

D = 16384
BLOCK = 128
HOT = 8
COLD = 4


BETA_ONE = 0.9
BETA_TWO = 0.95
ADAM_EPS = 1e-08
LEARN_RATE = 0.01
DECAY = 0.1
CORRECT_ONE = 1.0 - 0.9**10
CORRECT_TWO = 1.0 - 0.95**10


def from_behind(block, axis, distance):
    devices = range(lax.axis_size(axis))
    route = [((i - distance) % len(devices), i) for i in devices]
    return lax.ppermute(block, axis, route)


def pick_blocks(tok_rows, block_row):
    shaped = tok_rows.reshape(tok_rows.shape[0], D // BLOCK, BLOCK)
    return shaped[:, block_row, :].reshape(tok_rows.shape[0], block_row.shape[0] * BLOCK)


def per_device(activations, out_grad, block_ids, owner_map, master, moment, second):
    qlocal = out_grad.shape[1]
    hot_count = HOT * BLOCK
    outgoing = jax.vmap(lambda block_row: pick_blocks(activations, block_row))(block_ids)
    received = lax.all_to_all(outgoing, "tensor", split_axis=0, concat_axis=0, tiled=True)
    chosen = received.reshape(received.shape[0] * received.shape[1], received.shape[2])
    hot_cols = chosen[:, :hot_count]
    cold_cols = chosen[:, hot_count:]
    contract = (((0,), (0,)), ((), ()))
    grad = lax.psum_scatter(
        lax.dot_general(hot_cols, out_grad, contract, preferred_element_type=jnp.float32).astype(
            jnp.bfloat16
        ),
        "dp",
        scatter_dimension=0,
        tiled=True,
    ).astype(jnp.float32)
    cold_part = lax.dot_general(cold_cols, out_grad, contract, preferred_element_type=jnp.float32)
    cold_part = cold_part.astype(jnp.bfloat16).reshape(COLD, BLOCK * qlocal)
    new_moment = BETA_ONE * moment + (1.0 - BETA_ONE) * grad
    new_second = BETA_TWO * second + (1.0 - BETA_TWO) * grad * grad
    update = new_moment / CORRECT_ONE / (jnp.sqrt(new_second / CORRECT_TWO) + ADAM_EPS)
    new_master = master - LEARN_RATE * (update + DECAY * master)
    hot_weights = lax.all_gather(new_master.astype(jnp.bfloat16), "tensor", axis=1, tiled=True)
    dp_index = lax.axis_index("dp")
    dp_count = lax.axis_size("dp")
    prev_owner = lax.dynamic_index_in_dim(
        owner_map, (dp_index + dp_count - 1) % dp_count, 0, keepdims=False
    )
    next_owner = lax.dynamic_index_in_dim(owner_map, (dp_index + 1) % dp_count, 0, keepdims=False)
    from_prev = from_behind(cold_part, "dp", 1)
    from_next = from_behind(cold_part, "dp", -1)
    total = jnp.where((prev_owner == 1)[:, None], from_prev.astype(jnp.float32), 0.0)
    total = total + jnp.where((next_owner == 0)[:, None], from_next.astype(jnp.float32), 0.0)
    cold_recv = total.reshape(COLD * BLOCK, qlocal)
    return (new_master, new_moment, new_second, hot_weights, cold_recv)


def solution(mesh):
    return jax.shard_map(
        per_device,
        mesh=mesh,
        in_specs=(
            P(("dp", "tensor"), None),
            P("dp", "tensor"),
            P(),
            P(),
            P("dp", "tensor"),
            P("dp", "tensor"),
            P("dp", "tensor"),
        ),
        out_specs=(
            P("dp", "tensor"),
            P("dp", "tensor"),
            P("dp", "tensor"),
            P("dp", None),
            P("dp", "tensor"),
        ),
        check_vma=False,
    )
```

profile of v0, /device:TPU:13, one launch (start us, length us, event | category | flops | bytes accessed | tf_op | source)
XLA Modules:
  0.0 259.5 jit_solution(1642637924187993049)
XLA Ops:
  7.2 0.0 copy-start
  7.2 0.0 reduce-scatter.2.cloned.1.call-start
  7.2 0.8 compare_select_fusion
  8.1 0.1 reshape.46
  8.2 4.1 %copy_bitcast_fusion = bf16[96,128,128]{2,0,1:T(8,128)(2,1)} fusion(bf16[96,16384]{1,0:T(8,128)(2,1)} %param.7), kind=kLoop, calls=%fused_computation.4 | loop fusion | bytes 6291456 | tf_op jit(solution)/shard_map/vmap()/reshape | solution.py:28
  12.3 3.6 %gather_fusion = bf16[48,96,128]{2,1,0:T(8,128)(2,1)} fusion(bf16[96,128,128]{2,0,1:T(8,128)(2,1)} %copy_bitcast_fusion, s32[1024]{0:T(1024)S(1)} %pad_clamp_fusion), kind=kCustom, calls=%fused_computation | custom fusion | bytes 2359488 | tf_op jit(solution)/shard_map/vmap()/gather | solution.py:29
  15.9 1.5 copy.19
  17.4 30.4 %all_to_all.5 = bf16[4,96,1536]{2,1,0:T(8,128)(2,1)S(1)} all-to-all(bf16[4,96,1536]{2,1,0:T(8,128)(2,1)S(1)} %bitcast.16), channel_id=1, replica_groups=mesh['dp'=8,'tensor'=4] {'tensor'}, dimensions={0} | all-to-all | bytes 2359296 | tf_op jit(solution)/shard_map/all_to_all | solution.py:36
  47.8 0.0 copy-start.3
  47.8 1.0 copy-done.3
  48.8 0.0 copy-done
  48.8 6.8 %convolution_convert_fusion = bf16[1024,4096]{1,0:T(8,128)(2,1)} fusion(bf16[384,4096]{1,0:T(8,128)(2,1)S(1)} %copy-done, bf16[384,1536]{1,0:T(8,128)(2,1)S(1)} %bitcast.17), kind=kOutput, calls=%fused_computation.2 | convolution fusion | flops 3225419776 | bytes 12320768 | tf_op jit(solution)/shard_map/dot_general | solution.py:42
  55.6 0.0 reduce-scatter.2.cloned.1.call-update
  55.6 0.0 all-gather.2.cloned.1.call-start
  55.7 5.4 %convolution_convert_fusion.1 = bf16[512,4096]{1,0:T(8,128)(2,1)} fusion(bf16[384,4096]{1,0:T(8,128)(2,1)S(1)} %copy-done, bf16[384,1536]{1,0:T(8,128)(2,1)} %bitcast.18), kind=kOutput, calls=%fused_computation.3 | convolution fusion | flops 1612709888 | bytes 7733248 | tf_op jit(solution)/shard_map/dot_general | solution.py:49
  61.0 0.0 copy-start.4
  61.0 0.0 copy-start.2
  61.0 7.9 %reshape.42 = bf16[4,524288]{1,0:T(4,128)(2,1)} reshape(bf16[512,4096]{1,0:T(8,128)(2,1)} %convolution_convert_fusion.1) | data formatting | bytes 8388608 | tf_op jit(solution)/shard_map/reshape | solution.py:50
  68.9 2.6 collective-permute-start.1
  71.5 1.1 collective-permute-start
  72.6 0.0 copy-done.4
  72.6 0.2 fusion.4
  72.8 90.1 %reduce-scatter.2.cloned.1.call-done = bf16[128,4096]{1,0:T(8,128)(2,1)} async-done(((bf16[1024,4096]{1,0:T(8,128)(2,1)}), bf16[128,4096]{1,0:T(8,128)(2,1)}) %reduce-scatter.2.cloned.1.call-update) | async-done | bytes 1048592 | tf_op jit(solution)/shard_map/reduce_scatter | solution.py:41
  162.9 0.0 copy-done.2
  162.9 6.7 %fusion.6 = (bf16[128,4096]{1,0:T(8,128)(2,1)}, f32[128,4096]{1,0:T(8,128)}, f32[128,4096]{1,0:T(8,128)}, f32[128,4096]{1,0:T(8,128)}) fusion(f32[128,4096]{1,0:T(8,128)S(1)} %copy-done.2, bf16[128,4096]{1,0:T(8,128)(2,1)} %reduce-scatter.2.cloned.1.call-done, f32[128,4096]{1,0:T(8,128)} %param.12, f32[128,4096]{1,0:T(8,128)} %param.13), kind=kLoop, calls=%fused_computation.19 | loop fusion | flops 8912896 | bytes 14680064 | tf_op jit(solution)/shard_map/convert_element_type | solution.py:55
  169.6 0.0 all-gather.2.cloned.1.call-update
  169.6 28.3 %collective-permute-done.1 = bf16[4,524288]{1,0:T(4,128)(2,1)} collective-permute-done((bf16[4,524288]{1,0:T(4,128)(2,1)}, bf16[4,524288]{1,0:T(4,128)(2,1)}, u32[]{:S(2)}, u32[]{:S(2)}) %collective-permute-start.1) | collective-permute-done | bytes 4194336 | tf_op jit(solution)/shard_map/ppermute | solution.py:24
  198.0 0.0 collective-permute-done
  198.0 8.4 %select_add_fusion = f32[4,524288]{1,0:T(4,128)} fusion(bf16[4,524288]{1,0:T(4,128)(2,1)} %collective-permute-done.1, bf16[4,524288]{1,0:T(4,128)(2,1)} %collective-permute-done, pred[4]{0:T(512)(128)(4,1)S(1)} %get-tuple-element.6, pred[4]{0:T(512)(128)(4,1)S(1)} %get-tuple-element.5), kind=kLoop, calls=%fused_computation.1 | loop fusion | flops 10485760 | bytes 16777224 | tf_op jit(solution)/shard_map/add | solution.py:65
  206.4 12.6 %reshape.43 = f32[512,4096]{1,0:T(8,128)} reshape(f32[4,524288]{1,0:T(4,128)} %select_add_fusion) | data formatting | bytes 16777216 | tf_op jit(solution)/shard_map/reshape | solution.py:66
  219.0 29.0 %all-gather.2.cloned.1.call-done = bf16[128,16384]{1,0:T(8,128)(2,1)} async-done(((bf16[128,4096]{1,0:T(8,128)(2,1)}), bf16[128,16384]{1,0:T(8,128)(2,1)}) %all-gather.2.cloned.1.call-update) | async-done | bytes 4194320 | tf_op jit(solution)/shard_map/all_gather | solution.py:55
  247.9 0.0 copy-start.1
  247.9 4.7 %copy.21 = bf16[128,16384]{1,0:T(8,128)(2,1)} copy(bf16[128,16384]{1,0:T(8,128)(2,1)} %all-gather.2.cloned.1.call-done) | data formatting | bytes 8388608
  252.6 0.0 copy-done.1
  (1 shorter events, 0.0 us)
Async XLA Ops:
  7.2 41.6 %copy-start = (bf16[384,4096]{1,0:T(8,128)(2,1)S(1)}, bf16[384,4096]{1,0:T(8,128)(2,1)}, u32[]{:S(2)}) copy-start(bf16[384,4096]{1,0:T(8,128)(2,1)} %param.8) | copy-start | bytes 9437188
  7.2 155.7 %reduce-scatter.2.cloned.1.call-start = ((), (), s32[]{:S(2)}) async-start(), calls=%async_computation.2 | async-start | bytes 9437184 | tf_op jit(solution)/shard_map/reduce_scatter | solution.py:41
  47.8 1.0 copy-start.3
  55.6 192.3 %all-gather.2.cloned.1.call-start = ((), (), s32[]{:S(2)}) async-start(), calls=%async_computation.3 | async-start | bytes 5242880 | tf_op jit(solution)/shard_map/all_gather | solution.py:55
  61.0 11.5 %copy-start.4 = (s32[8,4]{0,1:T(4,128)S(1)}, s32[8,4]{0,1:T(4,128)}, u32[]{:S(2)}) copy-start(s32[8,4]{0,1:T(4,128)} %param.10) | copy-start | bytes 388
  61.0 101.9 %copy-start.2 = (f32[128,4096]{1,0:T(8,128)S(1)}, f32[128,4096]{1,0:T(8,128)}, u32[]{:S(2)}) copy-start(f32[128,4096]{1,0:T(8,128)} %param.11) | copy-start | bytes 6291460
  68.9 129.1 %collective-permute-start.1 = (bf16[4,524288]{1,0:T(4,128)(2,1)}, bf16[4,524288]{1,0:T(4,128)(2,1)}, u32[]{:S(2)}, u32[]{:S(2)}) collective-permute-start(bf16[4,524288]{1,0:T(4,128)(2,1)} %reshape.42), channel_id=1, source_target_pairs={{4,0},{8,4},{12,8},{16,12},{20,16},{24,20},{28,24},{0,28},{5,1},{9... | collective-permute-start | bytes 12582920 | tf_op jit(solution)/shard_map/ppermute | solution.py:24
  71.5 126.5 %collective-permute-start = (bf16[4,524288]{1,0:T(4,128)(2,1)}, bf16[4,524288]{1,0:T(4,128)(2,1)}, u32[]{:S(2)}, u32[]{:S(2)}) collective-permute-start(bf16[4,524288]{1,0:T(4,128)(2,1)} %reshape.42), channel_id=1, source_target_pairs={{28,0},{0,4},{4,8},{8,12},{12,16},{16,20},{20,24},{24,28},{29,1},{... | collective-permute-start | bytes 12582920 | tf_op jit(solution)/shard_map/ppermute | solution.py:24
  247.9 4.7 %copy-start.1 = (bf16[384,4096]{1,0:T(8,128)(2,1)S(1)}, bf16[384,4096]{1,0:T(8,128)(2,1)}, u32[]{:S(2)}) copy-start(bf16[384,4096]{1,0:T(8,128)(2,1)} %param.8) | copy-start | bytes 9437188
Sparse Core Ops, SparseCore 0:
  55.7 107.1 reduce-scatter.1
  169.8 78.1 all-gather.1
where the time goes:
time: 264 us; the launch traced here: 259 us
  waiting for transfers between devices  147 us (56%)
  local copies, waits for them, and re-layouts  35.5 us (13%)
  blocking collectives  30.4 us (12%)
  other arithmetic  16.1 us (6%)
  between operations  14.1 us (5%)
  matrix products  12.2 us (5%)
  starting transfers between devices  3.73 us (1%)
    reduce_scatter x1, waiting for transfers between devices, per_device(): lax.psum_scatter(lax.dot_general(hot_cols, out_grad, contract, preferred_...  90.1 us
    all_to_all x1, blocking collectives, per_device(): lax.all_to_all(outgoing, 'tensor', split_axis=0, concat_axis=0, tiled=True)  30.4 us
    all_gather x1, waiting for transfers between devices, per_device(): lax.all_gather(new_master.astype(jnp.bfloat16), 'tensor', axis=1, tiled=T...  29 us
    ppermute x2, waiting for transfers between devices, from_behind(): return lax.ppermute(block, axis, route)  28.3 us
    reshape x1, local copies, waits for them, and re-layouts, per_device(): cold_recv = total.reshape(COLD * BLOCK, qlocal)  12.6 us
    add x1, other arithmetic, per_device(): total + jnp.where((next_owner == 0)[:, None], from_next.astype(jnp.float3...  8.37 us
    reshape x1, local copies, waits for them, and re-layouts, per_device(): cold_part = cold_part.astype(jnp.bfloat16).reshape(COLD, BLOCK * qlocal)  7.89 us
    dot_general x1, matrix products, per_device(): lax.dot_general(hot_cols, out_grad, contract, preferred_element_type=jnp....  6.78 us
  transfers between devices with their start and end apart: 4, of which 3 were waited for; matrix products, arithmetic and copies ran while one was open for 16% of the time, Pallas kernels for 0%

commit v1 on v0

v1 whole, which is shorter than its diff:
```python
import functools

import jax
import jax.numpy as jnp
from jax import lax
from jax.experimental import pallas as pl
from jax.experimental.pallas import tpu as pltpu
from jax.sharding import PartitionSpec as P

BLOCK = 128
HOT = 8
COLD = 4
MOSTC = 3

BETA_ONE = 0.9
BETA_TWO = 0.95
ADAM_EPS = 1e-08
LEARN_RATE = 0.01
DECAY = 0.1
CORRECT_ONE = 1.0 - 0.9**10
CORRECT_TWO = 1.0 - 0.95**10

CHUNKS = 4
MESH = pl.DeviceIdType.MESH
F32 = jnp.float32
BF16 = jnp.bfloat16


def adam(grad, master, moment, second):
    new_moment = BETA_ONE * moment + (1.0 - BETA_ONE) * grad
    new_second = BETA_TWO * second + (1.0 - BETA_TWO) * grad * grad
    update = new_moment / CORRECT_ONE / (jnp.sqrt(new_second / CORRECT_TWO) + ADAM_EPS)
    return master - LEARN_RATE * (update + DECAY * master), new_moment, new_second


def halvings(n_dp):
    bits = []
    bit = n_dp // 2
    while bit >= 2:
        bits.append(bit)
        bit //= 2
    return bits


def flip(d, bit):
    return d + bit - 2 * bit * ((d // bit) % 2)


def gather_kernel(n_dp, n_t, unit, ids_ref, owner_ref, act, outbox, cold_outbox):
    i = lax.axis_index("dp")
    t = lax.axis_index("tensor")
    peer = flip(i, 1)
    bits = halvings(n_dp)
    half = outbox.shape[4] // unit

    owned = [owner_ref[i, c] for c in range(COLD)]
    ones = owned[0]
    for c in range(1, COLD):
        ones = ones + owned[c]
    place, taken, left = [], 0, ones
    for c in range(COLD):
        place.append(jnp.where(owned[c] == 1, taken, left))
        taken, left = taken + owned[c], left + 1 - owned[c]

    def column(block):
        return act[:, pl.ds(pl.multiple_of(block * BLOCK, BLOCK), BLOCK)]

    def hot_unit(group, d):
        index = (d * unit) // BLOCK
        cols = column(ids_ref[group, index])
        if unit < BLOCK:
            share = BLOCK // unit
            picked = cols[:, :unit]
            for s in range(1, share):
                picked = jnp.where(d % share == s, cols[:, s * unit : (s + 1) * unit], picked)
            cols = picked
        return cols

    for who, base in ((0, i), (1, peer)):
        for part in range(2):
            for k in range(n_t):
                group = (t + k) % n_t
                for u in range(half):
                    r = 2 * (u + half * (1 - part))
                    d = base
                    for b in bits:
                        if r & b:
                            d = flip(d, b)
                    cols = hot_unit(group, d)
                    outbox[who, part, k, :, pl.ds(u * unit, unit)] = cols
    for k in range(n_t):
        group = (t + k) % n_t
        for p in range(COLD):
            block = 0
            for c in range(COLD):
                block = block + jnp.where(place[c] == p, ids_ref[group, HOT + c], 0)
            cold_outbox[k, :, pl.ds(p * BLOCK, BLOCK)] = column(block)


def gather(n_dp, n_t, unit, ids, owner_map, activations):
    rows_tok = activations.shape[0]
    half = max(n_dp // 4, 1)
    smem = pl.BlockSpec(memory_space=pltpu.SMEM)
    vmem = pl.BlockSpec(memory_space=pltpu.VMEM)
    return pl.pallas_call(
        functools.partial(gather_kernel, n_dp, n_t, unit),
        out_shape=(
            jax.ShapeDtypeStruct((2, 2, n_t, rows_tok, half * unit), BF16),
            jax.ShapeDtypeStruct((n_t, rows_tok, COLD * BLOCK), BF16),
        ),
        in_specs=[smem, smem, vmem],
        out_specs=[vmem, vmem],
    )(ids, owner_map, activations)


def exchange_kernel(
    n_dp,
    n_t,
    outbox,
    cold_outbox,
    og_hbm,
    master_hbm,
    moment_hbm,
    second_hbm,
    grad_out,
    hot_out,
    prev_out,
    next_out,
    inbox,
    cold_inbox,
    og,
    lhs,
    cold_lhs,
    acc,
    rs_send,
    rs_recv,
    cold_send,
    master,
    moment,
    second,
    grad,
    hot_send,
    load_sem,
    sel_send_sem,
    sel_recv_sem,
    og_send_sem,
    og_recv_sem,
    rs_send_sem,
    rs_recv_sem,
    cold_send_sem,
    cold_recv_sem,
    hot_send_sem,
    hot_recv_sem,
    out_sem,
):
    i = lax.axis_index("dp")
    t = lax.axis_index("tensor")
    peer = flip(i, 1)
    rows_tok = cold_outbox.shape[1]
    tok, qlocal = og.shape[0] // 2, og.shape[1]
    units = n_dp // 2
    unit = grad.shape[0]
    half = max(units // 2, 1)
    hw = half * unit
    chunk = qlocal // CHUNKS

    loads = [
        pltpu.make_async_copy(og_hbm, og.at[pl.ds(0, tok)], load_sem.at[0]),
        pltpu.make_async_copy(master_hbm, master, load_sem.at[1]),
        pltpu.make_async_copy(moment_hbm, moment, load_sem.at[2]),
        pltpu.make_async_copy(second_hbm, second, load_sem.at[3]),
    ]
    loads[0].start()

    bits = halvings(n_dp)
    nxt, prv = (i + 1) % n_dp, (i + n_dp - 1) % n_dp
    partners = [(flip(i, b), t) for b in bits] + [(nxt, t), (prv, t), (peer, t)]
    for k in range(1, n_t):
        partners += [(i, (t + k) % n_t), (peer, (t + k) % n_t)]
    barrier = pltpu.get_barrier_semaphore()
    for partner in partners:
        pl.semaphore_signal(barrier, inc=1, device_id=partner, device_id_type=MESH)

    mine = pl.ds(t * rows_tok, rows_tok)
    for part in range(2):
        inbox[part, 0, mine, :] = outbox[0, part, 0]
    cold_inbox[mine, :] = cold_outbox[0]

    pl.semaphore_wait(barrier, len(partners))

    def sel_copy(who, part, k):
        return pltpu.make_async_remote_copy(
            src_ref=outbox.at[who, part, k],
            dst_ref=inbox.at[part, who, pl.ds(t * rows_tok, rows_tok)],
            send_sem=sel_send_sem.at[who, part, k],
            recv_sem=sel_recv_sem.at[who, part, k],
            device_id=(i if who == 0 else peer, (t + k) % n_t),
            device_id_type=MESH,
        )

    def cold_sel_copy(k):
        return pltpu.make_async_remote_copy(
            src_ref=cold_outbox.at[k],
            dst_ref=cold_inbox.at[pl.ds(t * rows_tok, rows_tok)],
            send_sem=sel_send_sem.at[0, 2, k],
            recv_sem=sel_recv_sem.at[0, 2, k],
            device_id=(i, (t + k) % n_t),
            device_id_type=MESH,
        )

    sel = {0: [], 1: [], 2: []}
    for part in range(2):
        for k in range(n_t):
            for who in range(2):
                if who or k:
                    sel[part].append(sel_copy(who, part, k))
    for k in range(1, n_t):
        sel[2].append(cold_sel_copy(k))
    og_copy = pltpu.make_async_remote_copy(
        src_ref=og_hbm,
        dst_ref=og.at[pl.ds(tok, tok)],
        send_sem=og_send_sem,
        recv_sem=og_recv_sem,
        device_id=(peer, t),
        device_id_type=MESH,
    )
    for copy in sel[0]:
        copy.start()
    og_copy.start()
    for part in (2, 1):
        for copy in sel[part]:
            copy.start()
    for load in loads[1:]:
        load.start()

    counts = [b // 2 for b in bits]
    offset = [sum(counts[:s]) * unit for s in range(len(bits))]

    def rs_copy(s, q):
        place_ = (pl.ds(offset[s], counts[s] * unit), pl.ds(q * chunk, chunk))
        return pltpu.make_async_remote_copy(
            src_ref=rs_send.at[place_],
            dst_ref=rs_recv.at[place_],
            send_sem=rs_send_sem.at[s, q],
            recv_sem=rs_recv_sem.at[s, q],
            device_id=(flip(i, bits[s]), t),
            device_id_type=MESH,
        )

    tile = min(512, chunk)

    def product(lhs_value_ref, rows, depth, col):
        return jnp.dot(
            lhs_value_ref[rows, :],
            og[pl.ds(0, depth), pl.ds(col, tile)],
            preferred_element_type=F32,
        )

    def wait_sel(part):
        for copy in sel[part]:
            copy.wait_recv()

    wait_sel(0)
    lhs[0, :, pl.ds(0, tok)] = inbox[0, 0].T
    lhs[0, :, pl.ds(tok, tok)] = inbox[0, 1].T
    loads[0].wait()
    og_copy.wait_recv()
    for q in range(CHUNKS):

        @pl.loop(0, chunk // tile)
        def _(n):
            col = pl.multiple_of(q * chunk + n * tile, tile)
            rs_send[pl.ds(0, hw), pl.ds(col, tile)] = product(
                lhs.at[0], slice(None), 2 * tok, col
            ).astype(BF16)

        rs_copy(0, q).start()

    def cold_copy(p, ahead, q):
        slot = p if ahead else p - 1
        place_ = (slot, slice(None), pl.ds(q * chunk, chunk))
        which = 0 if ahead else 1
        return pltpu.make_async_remote_copy(
            src_ref=cold_send.at[p, :, pl.ds(q * chunk, chunk)],
            dst_ref=(prev_out if ahead else next_out).at[place_],
            send_sem=cold_send_sem.at[which, slot, q],
            recv_sem=cold_recv_sem.at[which, slot, q],
            device_id=(nxt if ahead else prv, t),
            device_id_type=MESH,
        )

    wait_sel(2)
    cold_lhs[...] = cold_inbox[...].T
    for q in range(CHUNKS):

        @pl.loop(0, chunk // tile)
        def _(n):
            col = pl.multiple_of(q * chunk + n * tile, tile)
            out = product(cold_lhs, slice(None), tok, col).astype(BF16)
            for p in range(COLD):
                cold_send[p, :, pl.ds(col, tile)] = out[p * BLOCK : (p + 1) * BLOCK]

    def send_cold(q):
        for slot in range(MOSTC):
            cold_copy(slot, True, q).start()
            cold_copy(slot + COLD - MOSTC, False, q).start()

    send_cold(0)
    wait_sel(1)
    lhs[1, :, pl.ds(0, tok)] = inbox[1, 0].T
    lhs[1, :, pl.ds(tok, tok)] = inbox[1, 1].T

    @pl.loop(0, qlocal // tile)
    def _(n):
        col = pl.multiple_of(n * tile, tile)
        acc[:, pl.ds(col, tile)] = product(lhs.at[1], slice(None), 2 * tok, col)

    for load in loads[1:]:
        load.wait()

    def hot_copy(k, q):
        return pltpu.make_async_remote_copy(
            src_ref=hot_send.at[:, pl.ds(q * chunk, chunk)],
            dst_ref=hot_out.at[:, pl.ds(t * qlocal + q * chunk, chunk)],
            send_sem=hot_send_sem.at[k, q],
            recv_sem=hot_recv_sem.at[k, q],
            device_id=(i, (t + k) % n_t),
            device_id_type=MESH,
        )

    def grad_store(q):
        cols = pl.ds(q * chunk, chunk)
        return pltpu.make_async_copy(grad.at[:, cols], grad_out.at[:, cols], out_sem.at[0, q])

    def hot_store(q):
        return pltpu.make_async_copy(
            hot_send.at[:, pl.ds(q * chunk, chunk)],
            hot_out.at[:, pl.ds(t * qlocal + q * chunk, chunk)],
            out_sem.at[1, q],
        )

    step = min(256, chunk)

    def settle(s, q):
        rs_copy(s, q).wait_recv()
        last = s == len(bits) - 1

        @pl.loop(0, chunk // step)
        def _(n):
            cols = pl.ds(pl.multiple_of(q * chunk + n * step, step), step)
            keep = counts[s] * unit
            got = rs_recv[pl.ds(offset[s], keep), cols].astype(F32)
            total = acc[pl.ds(0, keep), cols] + got
            if last:
                grad[:, cols] = total
                new_master, _, _ = adam(total, master[:, cols], moment[:, cols], second[:, cols])
                hot_send[:, cols] = new_master.astype(BF16)
            else:
                sent = counts[s + 1] * unit
                acc[pl.ds(0, sent), cols] = total[:sent]
                rs_send[pl.ds(offset[s + 1], sent), cols] = total[sent:].astype(BF16)

        if last:
            for k in range(1, n_t):
                hot_copy(k, q).start()
            grad_store(q).start()
            hot_store(q).start()
        else:
            rs_copy(s + 1, q).start()

    cold_sent = 1
    for wave in range(CHUNKS + len(bits) - 1):
        for s in reversed(range(len(bits))):
            q = wave - s
            if 0 <= q < CHUNKS:
                settle(s, q)
        if cold_sent < CHUNKS:
            send_cold(cold_sent)
            cold_sent += 1

    for part in range(3):
        for copy in sel[part]:
            copy.wait_send()
    og_copy.wait_send()
    for q in range(CHUNKS):
        for s in range(len(bits)):
            rs_copy(s, q).wait_send()
        grad_store(q).wait()
        hot_store(q).wait()
        for k in range(1, n_t):
            hot_copy(k, q).wait()
        for slot in range(MOSTC):
            cold_copy(slot, True, q).wait()
            cold_copy(slot + COLD - MOSTC, False, q).wait()


def exchange(n_dp, n_t, outbox, cold_outbox, out_grad, master, moment, second):
    tok, qlocal = out_grad.shape
    unit = master.shape[0]
    units = n_dp // 2
    half = max(units // 2, 1)
    stages = max(n_dp.bit_length() - 2, 1)
    traded = (units - 1) * unit
    vmem = pl.BlockSpec(memory_space=pltpu.VMEM)
    anywhere = pl.BlockSpec(memory_space=pl.ANY)
    dma = pltpu.SemaphoreType.DMA
    return pl.pallas_call(
        functools.partial(exchange_kernel, n_dp, n_t),
        out_shape=(
            jax.ShapeDtypeStruct((unit, qlocal), F32),
            jax.ShapeDtypeStruct((unit, qlocal * n_t), BF16),
            jax.ShapeDtypeStruct((MOSTC, BLOCK, qlocal), BF16),
            jax.ShapeDtypeStruct((MOSTC, BLOCK, qlocal), BF16),
        ),
        in_specs=[vmem, vmem] + [anywhere] * 4,
        out_specs=[anywhere] * 4,
        scratch_shapes=[
            pltpu.VMEM((2, 2, tok, half * unit), BF16),
            pltpu.VMEM((tok, COLD * BLOCK), BF16),
            pltpu.VMEM((2 * tok, qlocal), BF16),
            pltpu.VMEM((2, half * unit, 2 * tok), BF16),
            pltpu.VMEM((COLD * BLOCK, tok), BF16),
            pltpu.VMEM((half * unit, qlocal), F32),
            pltpu.VMEM((traded, qlocal), BF16),
            pltpu.VMEM((traded, qlocal), BF16),
            pltpu.VMEM((COLD, BLOCK, qlocal), BF16),
            pltpu.VMEM((unit, qlocal), F32),
            pltpu.VMEM((unit, qlocal), F32),
            pltpu.VMEM((unit, qlocal), F32),
            pltpu.VMEM((unit, qlocal), F32),
            pltpu.VMEM((unit, qlocal), BF16),
            dma((4,)),
            dma((2, 3, n_t)),
            dma((2, 3, n_t)),
            dma(()),
            dma(()),
            dma((stages, CHUNKS)),
            dma((stages, CHUNKS)),
            dma((2, MOSTC, CHUNKS)),
            dma((2, MOSTC, CHUNKS)),
            dma((n_t, CHUNKS)),
            dma((n_t, CHUNKS)),
            dma((2, CHUNKS)),
        ],
        compiler_params=pltpu.CompilerParams(
            collective_id=0, has_side_effects=True, vmem_limit_bytes=60 * 1024 * 1024
        ),
    )(outbox, cold_outbox, out_grad, master, moment, second)


def cold_kernel(where_ref, owner_ref, prev_ref, next_ref, out_ref):
    c = pl.program_id(0)
    from_prev = owner_ref[where_ref[0], c] == 1
    from_next = owner_ref[where_ref[1], c] == 0
    total = jnp.where(from_prev, prev_ref[0].astype(F32), 0.0)
    out_ref[...] = total + jnp.where(from_next, next_ref[0].astype(F32), 0.0)


def ones_before(owner_ref, row, c):
    count = 0
    for b in range(COLD):
        count = count + jnp.where(b < c, owner_ref[row, b], 0)
    return count


def prev_slot(c, n, where_ref, owner_ref):
    return jnp.minimum(ones_before(owner_ref, where_ref[0], c), MOSTC - 1), 0, n


def next_slot(c, n, where_ref, owner_ref):
    row = where_ref[1]
    ones = ones_before(owner_ref, row, COLD)
    place = ones + c - ones_before(owner_ref, row, c)
    return jnp.clip(place - (COLD - MOSTC), 0, MOSTC - 1), 0, n


def merge_cold(where, owner_map, from_prev, from_next):
    qlocal = from_prev.shape[2]
    width = qlocal // 2
    return pl.pallas_call(
        cold_kernel,
        out_shape=jax.ShapeDtypeStruct((COLD * BLOCK, qlocal), F32),
        grid_spec=pltpu.PrefetchScalarGridSpec(
            num_scalar_prefetch=2,
            grid=(COLD, 2),
            in_specs=[
                pl.BlockSpec((1, BLOCK, width), prev_slot),
                pl.BlockSpec((1, BLOCK, width), next_slot),
            ],
            out_specs=pl.BlockSpec((BLOCK, width), lambda c, n, *_: (c, n)),
        ),
    )(where, owner_map, from_prev, from_next)


def per_device(n_dp, n_t, activations, out_grad, block_ids, owner_map, master, moment, second):
    outbox, cold_outbox = gather(n_dp, n_t, master.shape[0], block_ids, owner_map, activations)
    grad, hot_weights, from_prev, from_next = exchange(
        n_dp, n_t, outbox, cold_outbox, out_grad, master, moment, second
    )
    index = lax.axis_index("dp")
    where = jnp.stack([(index + n_dp - 1) % n_dp, (index + 1) % n_dp]).astype(jnp.int32)
    cold_recv = merge_cold(where, owner_map, from_prev, from_next)
    new_master, new_moment, new_second = adam(grad, master, moment, second)
    return (new_master, new_moment, new_second, hot_weights, cold_recv)


def solution(mesh):
    return jax.shard_map(
        functools.partial(per_device, mesh.shape["dp"], mesh.shape["tensor"]),
        mesh=mesh,
        in_specs=(
            P(("dp", "tensor"), None),
            P("dp", "tensor"),
            P(),
            P(),
            P("dp", "tensor"),
            P("dp", "tensor"),
            P("dp", "tensor"),
        ),
        out_specs=(
            P("dp", "tensor"),
            P("dp", "tensor"),
            P("dp", "tensor"),
            P("dp", None),
            P("dp", "tensor"),
        ),
        check_vma=False,
    )
```

time: 264 us -> 173 us (0.66)
  Pallas kernels: 0 us -> 159 us
  waiting for transfers between devices: 147 us -> 0 us
  local copies, waits for them, and re-layouts: 35.5 us -> 3.37 us
  blocking collectives: 30.4 us -> 0 us
  between operations: 14.1 us -> 0.67 us
  matrix products: 12.2 us -> 0 us
  other arithmetic: 16.1 us -> 7.48 us
  starting transfers between devices: 3.73 us -> 0 us
    pallas_call x0 -> x3, Pallas kernels: none -> 159 us  [the longest x1 146 us: exchange(): pl.pallas_call(functools.partial(exchange_kernel, n_dp, n_t), out_shape=(...]
    reduce_scatter x1 -> x0, waiting for transfers between devices: 90.1 us -> none  [per_device(): lax.psum_scatter(lax.dot_general(hot_cols, out_grad, contract, preferred_...]
    all_to_all x1 -> x0, blocking collectives: 30.4 us -> none  [per_device(): lax.all_to_all(outgoing, 'tensor', split_axis=0, concat_axis=0, tiled=True)]
    all_gather x1 -> x0, waiting for transfers between devices: 29 us -> none  [per_device(): lax.all_gather(new_master.astype(jnp.bfloat16), 'tensor', axis=1, tiled=T...]
    ppermute x2 -> x0, waiting for transfers between devices: 28.3 us -> none  [from_behind(): return lax.ppermute(block, axis, route)]
    reshape x4 -> x0, local copies, waits for them, and re-layouts: 26 us -> none  [the longest x1 12.6 us: per_device(): cold_recv = total.reshape(COLD * BLOCK, qlocal)]
    dot_general x2 -> x0, matrix products: 12.2 us -> none  [the longest x1 6.78 us: per_device(): lax.dot_general(hot_cols, out_grad, contract, preferred_element_type=jnp....]
    add x1 -> x0, other arithmetic: 8.37 us -> none  [per_device(): total + jnp.where((next_owner == 0)[:, None], from_next.astype(jnp.float3...]
  transfers between devices with their start and end apart: 4 -> 0, of which waited for: 3 -> 0; matrix products, arithmetic and copies ran while one was open for 16% -> 0% of each run, Pallas kernels for 0% -> 0%
where the time goes in v1:
time: 173 us; the launch traced here: 171 us
  Pallas kernels  159 us (92%)
  other arithmetic  7.48 us (4%)
  local copies, waits for them, and re-layouts  3.37 us (2%)
    pallas_call x1, Pallas kernels, exchange(): pl.pallas_call(functools.partial(exchange_kernel, n_dp, n_t), out_shape=(...  146 us
    pallas_call x1, Pallas kernels, merge_cold(): pl.pallas_call(cold_kernel, out_shape=jax.ShapeDtypeStruct((COLD * BLOCK,...  10.1 us
    sub x1, other arithmetic, adam(): master - LEARN_RATE * (update + DECAY * master)  6.89 us

profile of v1, /device:TPU:13, one launch (start us, length us, event | category | flops | bytes accessed | tf_op | source)
XLA Modules:
  0.0 170.7 jit_solution(8443720185881076120)
XLA Ops:
  0.7 0.6 pad_add_fusion.where_ref
  1.2 1.3 copy.12.owner_ref
  2.6 3.3 %shard_map.110 = (bf16[2,2,4,96,256]{4,3,2,1,0:T(8,128)(2,1)}, bf16[4,96,512]{2,1,0:T(8,128)(2,1)}) custom-call(s32[4,12]{1,0:T(4,128)} %ids_ref.1, s32[8,4]{1,0:T(8,128)} %copy.12.owner_ref, bf16[96,16384]{1,0:T(8,128)(2,1)} %act.1), custom_call_target="tpu_custom_call" | custom-call | tf_op jit(solution)/shard_map/pallas_call | solution.py:105
  5.8 145.8 %shard_map.111 = (f32[128,4096]{1,0:T(8,128)}, bf16[128,16384]{1,0:T(8,128)(2,1)}, bf16[3,128,4096]{2,1,0:T(8,128)(2,1)}, bf16[3,128,4096]{2,1,0:T(8,128)(2,1)}) custom-call(bf16[2,2,4,96,256]{4,3,2,1,0:T(8,128)(2,1)} %get-tuple-element.11.outbox, bf16[4,96,512]{2,1,0:T(8,128)(2,1)} %get-tuple-element.12.cold_outbox, bf16[384,4096]{1,0:T(8,128)(2,1)} %og_hbm.1, ...), custom_call_target="tpu_custom_call" | custom-call | tf_op jit(solution)/shard_map/pallas_call | solution.py:407
  151.7 0.0 copy-start
  151.7 10.1 %shard_map.112 = f32[512,4096]{1,0:T(8,128)} custom-call(s32[2]{0:T(128)} %pad_add_fusion.where_ref, s32[8,4]{1,0:T(8,128)} %copy.12.owner_ref, bf16[3,128,4096]{2,1,0:T(8,128)(2,1)} %get-tuple-element.15.prev_ref, bf16[3,128,4096]{2,1,0:T(8,128)(2,1)} %get-tuple-element.16.next_ref), custom_call_target="tpu_custom_call" | custom-call | tf_op jit(solution)/shard_map/pallas_call | solution.py:480
  161.8 0.0 copy-done
  161.8 0.0 copy-start.1
  161.8 6.9 %multiply_subtract_fusion = (f32[128,4096]{1,0:T(8,128)}, f32[128,4096]{1,0:T(8,128)}, f32[128,4096]{1,0:T(8,128)}) fusion(f32[128,4096]{1,0:T(8,128)S(1)} %copy-done, f32[128,4096]{1,0:T(8,128)} %get-tuple-element.13, f32[128,4096]{1,0:T(8,128)} %moment_hbm.1, f32[128,4096]{1,0:T(8,128)} %second_hbm.1), kind=kLoop, calls=%fused_computation.2 | loop fusion | flops 7864320 | bytes 14680064 | tf_op jit(solution)/shard_map/sub | solution.py:33
  168.7 0.0 copy-done.1
  168.7 2.0 %copy.15 = bf16[128,16384]{1,0:T(8,128)(2,1)} copy(bf16[128,16384]{1,0:T(8,128)(2,1)S(1)} %copy-done.1) | data formatting | bytes 8388608
Async XLA Ops:
  151.7 10.1 %copy-start = (f32[128,4096]{1,0:T(8,128)S(1)}, f32[128,4096]{1,0:T(8,128)}, u32[]{:S(2)}) copy-start(f32[128,4096]{1,0:T(8,128)} %master_hbm.1) | copy-start | bytes 6291460
  161.8 6.9 %copy-start.1 = (bf16[128,16384]{1,0:T(8,128)(2,1)S(1)}, bf16[128,16384]{1,0:T(8,128)(2,1)}, u32[]{:S(2)}) copy-start(bf16[128,16384]{1,0:T(8,128)(2,1)} %get-tuple-element.28) | copy-start | bytes 12582916

commit v2 on v1

--- a/solution.py
+++ b/solution.py
@@ -224,10 +224,8 @@
         device_id=(peer, t),
         device_id_type=MESH,
     )
-    for copy in sel[0]:
-        copy.start()
     og_copy.start()
-    for part in (2, 1):
+    for part in (2, 0, 1):
         for copy in sel[part]:
             copy.start()
     for load in loads[1:]:
@@ -259,22 +257,6 @@
     def wait_sel(part):
         for copy in sel[part]:
             copy.wait_recv()
-
-    wait_sel(0)
-    lhs[0, :, pl.ds(0, tok)] = inbox[0, 0].T
-    lhs[0, :, pl.ds(tok, tok)] = inbox[0, 1].T
-    loads[0].wait()
-    og_copy.wait_recv()
-    for q in range(CHUNKS):
-
-        @pl.loop(0, chunk // tile)
-        def _(n):
-            col = pl.multiple_of(q * chunk + n * tile, tile)
-            rs_send[pl.ds(0, hw), pl.ds(col, tile)] = product(
-                lhs.at[0], slice(None), 2 * tok, col
-            ).astype(BF16)
-
-        rs_copy(0, q).start()
 
     def cold_copy(p, ahead, q):
         slot = p if ahead else p - 1
@@ -291,6 +273,7 @@
 
     wait_sel(2)
     cold_lhs[...] = cold_inbox[...].T
+    loads[0].wait()
     for q in range(CHUNKS):
 
         @pl.loop(0, chunk // tile)
@@ -305,7 +288,27 @@
             cold_copy(slot, True, q).start()
             cold_copy(slot + COLD - MOSTC, False, q).start()
 
+    direct = (i % 4 == 1) | (i % 4 == 2)
     send_cold(0)
+    wait_sel(0)
+    lhs[0, :, pl.ds(0, tok)] = inbox[0, 0].T
+    lhs[0, :, pl.ds(tok, tok)] = inbox[0, 1].T
+    og_copy.wait_recv()
+    for q in range(CHUNKS):
+
+        @pl.loop(0, chunk // tile)
+        def _(n):
+            col = pl.multiple_of(q * chunk + n * tile, tile)
+            rs_send[pl.ds(0, hw), pl.ds(col, tile)] = product(
+                lhs.at[0], slice(None), 2 * tok, col
+            ).astype(BF16)
+
+        rs_copy(0, q).start()
+
+    @pl.when(direct)
+    def _():
+        send_cold(1)
+
     wait_sel(1)
     lhs[1, :, pl.ds(0, tok)] = inbox[1, 0].T
     lhs[1, :, pl.ds(tok, tok)] = inbox[1, 1].T
@@ -318,15 +321,32 @@
     for load in loads[1:]:
         load.wait()
 
-    def hot_copy(k, q):
+    def hot_copy(way, hop, q):
+        origin = t - hop if way == 0 else t + hop
+        cols = pl.ds(q * chunk, chunk)
+        place_ = (slice(None), pl.ds(origin * qlocal + q * chunk, chunk))
         return pltpu.make_async_remote_copy(
-            src_ref=hot_send.at[:, pl.ds(q * chunk, chunk)],
-            dst_ref=hot_out.at[:, pl.ds(t * qlocal + q * chunk, chunk)],
-            send_sem=hot_send_sem.at[k, q],
-            recv_sem=hot_recv_sem.at[k, q],
-            device_id=(i, (t + k) % n_t),
+            src_ref=hot_send.at[:, cols] if hop == 0 else hot_out.at[place_],
+            dst_ref=hot_out.at[place_],
+            send_sem=hot_send_sem.at[way, hop, q],
+            recv_sem=hot_recv_sem.at[way, hop, q],
+            device_id=(i, (t + 1) % n_t if way == 0 else (t + n_t - 1) % n_t),
             device_id_type=MESH,
         )
+
+    def can_send(way, hop):
+        if way == 0:
+            return (t >= hop) & (t < n_t - 1)
+        return (t + hop <= n_t - 1) & (t > 0)
+
+    def send_hot(hop, q):
+        for way in range(2):
+
+            @pl.when(can_send(way, hop))
+            def _():
+                if hop:
+                    hot_copy(way, hop - 1, q).wait_recv()
+                hot_copy(way, hop, q).start()
 
     def grad_store(q):
         cols = pl.ds(q * chunk, chunk)
@@ -361,22 +381,33 @@
                 rs_send[pl.ds(offset[s + 1], sent), cols] = total[sent:].astype(BF16)
 
         if last:
-            for k in range(1, n_t):
-                hot_copy(k, q).start()
+            send_hot(0, q)
             grad_store(q).start()
             hot_store(q).start()
         else:
             rs_copy(s + 1, q).start()
 
-    cold_sent = 1
-    for wave in range(CHUNKS + len(bits) - 1):
+    for wave in range(CHUNKS + len(bits) - 1 + n_t - 2):
         for s in reversed(range(len(bits))):
             q = wave - s
             if 0 <= q < CHUNKS:
                 settle(s, q)
-        if cold_sent < CHUNKS:
-            send_cold(cold_sent)
-            cold_sent += 1
+        if 1 <= wave < CHUNKS:
+
+            @pl.when(jnp.logical_not(direct))
+            def _():
+                send_cold(wave)
+
+        if 1 <= wave < CHUNKS - 1:
+
+            @pl.when(direct)
+            def _():
+                send_cold(wave + 1)
+
+        for hop in range(1, n_t - 1):
+            q = wave - (len(bits) - 1) - hop
+            if 0 <= q < CHUNKS:
+                send_hot(hop, q)
 
     for part in range(3):
         for copy in sel[part]:
@@ -387,8 +418,17 @@
             rs_copy(s, q).wait_send()
         grad_store(q).wait()
         hot_store(q).wait()
-        for k in range(1, n_t):
-            hot_copy(k, q).wait()
+        for hop in range(n_t - 1):
+            for way in range(2):
+
+                @pl.when(can_send(way, hop))
+                def _():
+                    hot_copy(way, hop, q).wait_send()
+
+                @pl.when((t == n_t - 1) if way == 0 else (t == 0))
+                def _():
+                    hot_copy(way, hop, q).wait_recv()
+
         for slot in range(MOSTC):
             cold_copy(slot, True, q).wait()
             cold_copy(slot + COLD - MOSTC, False, q).wait()
@@ -438,8 +478,8 @@
             dma((stages, CHUNKS)),
             dma((2, MOSTC, CHUNKS)),
             dma((2, MOSTC, CHUNKS)),
-            dma((n_t, CHUNKS)),
-            dma((n_t, CHUNKS)),
+            dma((2, n_t, CHUNKS)),
+            dma((2, n_t, CHUNKS)),
             dma((2, CHUNKS)),
         ],
         compiler_params=pltpu.CompilerParams(
@@ -476,13 +516,13 @@
 
 def merge_cold(where, owner_map, from_prev, from_next):
     qlocal = from_prev.shape[2]
-    width = qlocal // 2
+    width = qlocal // 4
     return pl.pallas_call(
         cold_kernel,
         out_shape=jax.ShapeDtypeStruct((COLD * BLOCK, qlocal), F32),
         grid_spec=pltpu.PrefetchScalarGridSpec(
             num_scalar_prefetch=2,
-            grid=(COLD, 2),
+            grid=(COLD, 4),
             in_specs=[
                 pl.BlockSpec((1, BLOCK, width), prev_slot),
                 pl.BlockSpec((1, BLOCK, width), next_slot),

time: 173 us -> 179 us (1.035)
  Pallas kernels: 159 us -> 164 us
    pallas_call x1, Pallas kernels: 10.1 us -> 13.1 us  [merge_cold(): pl.pallas_call(cold_kernel, out_shape=jax.ShapeDtypeStruct((COLD * BLOCK,...]
    pallas_call x1, Pallas kernels: 146 us -> 148 us  [exchange(): pl.pallas_call(functools.partial(exchange_kernel, n_dp, n_t), out_shape=(...]
where the time goes in v2:
time: 179 us; the launch traced here: 176 us
  Pallas kernels  164 us (92%)
  other arithmetic  7.48 us (4%)
  local copies, waits for them, and re-layouts  3.37 us (2%)
    pallas_call x1, Pallas kernels, exchange(): pl.pallas_call(functools.partial(exchange_kernel, n_dp, n_t), out_shape=(...  148 us
    pallas_call x1, Pallas kernels, merge_cold(): pl.pallas_call(cold_kernel, out_shape=jax.ShapeDtypeStruct((COLD * BLOCK,...  13.1 us
    sub x1, other arithmetic, adam(): master - LEARN_RATE * (update + DECAY * master)  6.89 us

profile of v2, /device:TPU:13, one launch (start us, length us, event | category | flops | bytes accessed | tf_op | source)
XLA Modules:
  0.0 176.0 jit_solution(908917358024095447)
XLA Ops:
  0.7 0.6 pad_add_fusion.where_ref
  1.2 1.3 copy.12.owner_ref
  2.6 3.3 %shard_map.110 = (bf16[2,2,4,96,256]{4,3,2,1,0:T(8,128)(2,1)}, bf16[4,96,512]{2,1,0:T(8,128)(2,1)}) custom-call(s32[4,12]{1,0:T(4,128)} %ids_ref.1, s32[8,4]{1,0:T(8,128)} %copy.12.owner_ref, bf16[96,16384]{1,0:T(8,128)(2,1)} %act.1), custom_call_target="tpu_custom_call" | custom-call | tf_op jit(solution)/shard_map/pallas_call | solution.py:105
  5.8 148.1 %shard_map.111 = (f32[128,4096]{1,0:T(8,128)}, bf16[128,16384]{1,0:T(8,128)(2,1)}, bf16[3,128,4096]{2,1,0:T(8,128)(2,1)}, bf16[3,128,4096]{2,1,0:T(8,128)(2,1)}) custom-call(bf16[2,2,4,96,256]{4,3,2,1,0:T(8,128)(2,1)} %get-tuple-element.11.outbox, bf16[4,96,512]{2,1,0:T(8,128)(2,1)} %get-tuple-element.12.cold_outbox, bf16[384,4096]{1,0:T(8,128)(2,1)} %og_hbm.1, ...), custom_call_target="tpu_custom_call" | custom-call | tf_op jit(solution)/shard_map/pallas_call | solution.py:447
  153.9 0.0 copy-start
  154.0 13.1 %shard_map.112 = f32[512,4096]{1,0:T(8,128)} custom-call(s32[2]{0:T(128)} %pad_add_fusion.where_ref, s32[8,4]{1,0:T(8,128)} %copy.12.owner_ref, bf16[3,128,4096]{2,1,0:T(8,128)(2,1)} %get-tuple-element.15.prev_ref, bf16[3,128,4096]{2,1,0:T(8,128)(2,1)} %get-tuple-element.16.next_ref), custom_call_target="tpu_custom_call" | custom-call | tf_op jit(solution)/shard_map/pallas_call | solution.py:520
  167.1 0.0 copy-done
  167.1 0.0 copy-start.1
  167.1 6.9 %multiply_subtract_fusion = (f32[128,4096]{1,0:T(8,128)}, f32[128,4096]{1,0:T(8,128)}, f32[128,4096]{1,0:T(8,128)}) fusion(f32[128,4096]{1,0:T(8,128)S(1)} %copy-done, f32[128,4096]{1,0:T(8,128)} %get-tuple-element.13, f32[128,4096]{1,0:T(8,128)} %moment_hbm.1, f32[128,4096]{1,0:T(8,128)} %second_hbm.1), kind=kLoop, calls=%fused_computation.2 | loop fusion | flops 7864320 | bytes 14680064 | tf_op jit(solution)/shard_map/sub | solution.py:33
  174.0 0.0 copy-done.1
  174.0 2.0 %copy.15 = bf16[128,16384]{1,0:T(8,128)(2,1)} copy(bf16[128,16384]{1,0:T(8,128)(2,1)S(1)} %copy-done.1) | data formatting | bytes 8388608
Async XLA Ops:
  153.9 13.1 %copy-start = (f32[128,4096]{1,0:T(8,128)S(1)}, f32[128,4096]{1,0:T(8,128)}, u32[]{:S(2)}) copy-start(f32[128,4096]{1,0:T(8,128)} %master_hbm.1) | copy-start | bytes 6291460
  167.1 6.9 %copy-start.1 = (bf16[128,16384]{1,0:T(8,128)(2,1)S(1)}, bf16[128,16384]{1,0:T(8,128)(2,1)}, u32[]{:S(2)}) copy-start(bf16[128,16384]{1,0:T(8,128)(2,1)} %get-tuple-element.28) | copy-start | bytes 12582916

commit v3 on v1

--- a/solution.py
+++ b/solution.py
@@ -20,7 +20,7 @@
 CORRECT_ONE = 1.0 - 0.9**10
 CORRECT_TWO = 1.0 - 0.95**10
 
-CHUNKS = 4
+CHUNKS = 8
 MESH = pl.DeviceIdType.MESH
 F32 = jnp.float32
 BF16 = jnp.bfloat16
@@ -227,9 +227,6 @@
     for copy in sel[0]:
         copy.start()
     og_copy.start()
-    for part in (2, 1):
-        for copy in sel[part]:
-            copy.start()
     for load in loads[1:]:
         load.start()
 
@@ -261,6 +258,9 @@
             copy.wait_recv()
 
     wait_sel(0)
+    for part in (2, 1):
+        for copy in sel[part]:
+            copy.start()
     lhs[0, :, pl.ds(0, tok)] = inbox[0, 0].T
     lhs[0, :, pl.ds(tok, tok)] = inbox[0, 1].T
     loads[0].wait()
@@ -305,7 +305,6 @@
             cold_copy(slot, True, q).start()
             cold_copy(slot + COLD - MOSTC, False, q).start()
 
-    send_cold(0)
     wait_sel(1)
     lhs[1, :, pl.ds(0, tok)] = inbox[1, 0].T
     lhs[1, :, pl.ds(tok, tok)] = inbox[1, 1].T
@@ -368,7 +367,7 @@
         else:
             rs_copy(s + 1, q).start()
 
-    cold_sent = 1
+    cold_sent = 0
     for wave in range(CHUNKS + len(bits) - 1):
         for s in reversed(range(len(bits))):
             q = wave - s
@@ -476,13 +475,13 @@
 
 def merge_cold(where, owner_map, from_prev, from_next):
     qlocal = from_prev.shape[2]
-    width = qlocal // 2
+    width = qlocal
     return pl.pallas_call(
         cold_kernel,
         out_shape=jax.ShapeDtypeStruct((COLD * BLOCK, qlocal), F32),
         grid_spec=pltpu.PrefetchScalarGridSpec(
             num_scalar_prefetch=2,
-            grid=(COLD, 2),
+            grid=(COLD, 1),
             in_specs=[
                 pl.BlockSpec((1, BLOCK, width), prev_slot),
                 pl.BlockSpec((1, BLOCK, width), next_slot),

time: 173 us -> 158 us (0.913)
  Pallas kernels: 159 us -> 146 us
    pallas_call x1, Pallas kernels: 146 us -> 134 us  [exchange(): pl.pallas_call(functools.partial(exchange_kernel, n_dp, n_t), out_shape=(...]
    pallas_call x1, Pallas kernels: 10.1 us -> 8.28 us  [merge_cold(): pl.pallas_call(cold_kernel, out_shape=jax.ShapeDtypeStruct((COLD * BLOCK,...]
where the time goes in v3:
time: 158 us; the launch traced here: 157 us
  Pallas kernels  146 us (92%)
  other arithmetic  7.48 us (5%)
  local copies, waits for them, and re-layouts  3.37 us (2%)
    pallas_call x1, Pallas kernels, exchange(): pl.pallas_call(functools.partial(exchange_kernel, n_dp, n_t), out_shape=(...  134 us
    pallas_call x1, Pallas kernels, merge_cold(): pl.pallas_call(cold_kernel, out_shape=jax.ShapeDtypeStruct((COLD * BLOCK,...  8.28 us
    sub x1, other arithmetic, adam(): master - LEARN_RATE * (update + DECAY * master)  6.89 us
    unnamed x6, local copies, waits for them, and re-layouts  3.37 us
    pallas_call x1, Pallas kernels, gather(): pl.pallas_call(functools.partial(gather_kernel, n_dp, n_t, unit), out_sha...  3.25 us

profile of v3, /device:TPU:13, one launch (start us, length us, event | category | flops | bytes accessed | tf_op | source)
XLA Modules:
  0.0 157.5 jit_solution(12534515412904382966)
XLA Ops:
  0.7 0.6 pad_add_fusion.where_ref
  1.2 1.3 copy.12.owner_ref
  2.6 3.3 %shard_map.110 = (bf16[2,2,4,96,256]{4,3,2,1,0:T(8,128)(2,1)}, bf16[4,96,512]{2,1,0:T(8,128)(2,1)}) custom-call(s32[4,12]{1,0:T(4,128)} %ids_ref.1, s32[8,4]{1,0:T(8,128)} %copy.12.owner_ref, bf16[96,16384]{1,0:T(8,128)(2,1)} %act.1), custom_call_target="tpu_custom_call" | custom-call | tf_op jit(solution)/shard_map/pallas_call | solution.py:105
  5.8 134.4 %shard_map.111 = (f32[128,4096]{1,0:T(8,128)}, bf16[128,16384]{1,0:T(8,128)(2,1)}, bf16[3,128,4096]{2,1,0:T(8,128)(2,1)}, bf16[3,128,4096]{2,1,0:T(8,128)(2,1)}) custom-call(bf16[2,2,4,96,256]{4,3,2,1,0:T(8,128)(2,1)} %get-tuple-element.11.outbox, bf16[4,96,512]{2,1,0:T(8,128)(2,1)} %get-tuple-element.12.cold_outbox, bf16[384,4096]{1,0:T(8,128)(2,1)} %og_hbm.1, ...), custom_call_target="tpu_custom_call" | custom-call | tf_op jit(solution)/shard_map/pallas_call | solution.py:406
  140.2 0.0 copy-start
  140.3 8.3 %shard_map.112 = f32[512,4096]{1,0:T(8,128)} custom-call(s32[2]{0:T(128)} %pad_add_fusion.where_ref, s32[8,4]{1,0:T(8,128)} %copy.12.owner_ref, bf16[3,128,4096]{2,1,0:T(8,128)(2,1)} %get-tuple-element.15.prev_ref, bf16[3,128,4096]{2,1,0:T(8,128)(2,1)} %get-tuple-element.16.next_ref), custom_call_target="tpu_custom_call" | custom-call | tf_op jit(solution)/shard_map/pallas_call | solution.py:479
  148.5 0.0 copy-done
  148.5 0.0 copy-start.1
  148.5 6.9 %multiply_subtract_fusion = (f32[128,4096]{1,0:T(8,128)}, f32[128,4096]{1,0:T(8,128)}, f32[128,4096]{1,0:T(8,128)}) fusion(f32[128,4096]{1,0:T(8,128)S(1)} %copy-done, f32[128,4096]{1,0:T(8,128)} %get-tuple-element.13, f32[128,4096]{1,0:T(8,128)} %moment_hbm.1, f32[128,4096]{1,0:T(8,128)} %second_hbm.1), kind=kLoop, calls=%fused_computation.2 | loop fusion | flops 7864320 | bytes 14680064 | tf_op jit(solution)/shard_map/sub | solution.py:33
  155.4 0.0 copy-done.1
  155.4 2.0 %copy.15 = bf16[128,16384]{1,0:T(8,128)(2,1)} copy(bf16[128,16384]{1,0:T(8,128)(2,1)S(1)} %copy-done.1) | data formatting | bytes 8388608
Async XLA Ops:
  140.2 8.3 %copy-start = (f32[128,4096]{1,0:T(8,128)S(1)}, f32[128,4096]{1,0:T(8,128)}, u32[]{:S(2)}) copy-start(f32[128,4096]{1,0:T(8,128)} %master_hbm.1) | copy-start | bytes 6291460
  148.5 6.9 %copy-start.1 = (bf16[128,16384]{1,0:T(8,128)(2,1)S(1)}, bf16[128,16384]{1,0:T(8,128)(2,1)}, u32[]{:S(2)}) copy-start(bf16[128,16384]{1,0:T(8,128)(2,1)} %get-tuple-element.28) | copy-start | bytes 12582916
